TPU v7x, 32 devices: a whole 2x2x4 slice. The times are simulated.
32 devices in a mesh: shard: 2 (over core), width: 4 (over y, x), shift: 4 (over z).
Axes of the slice: x: 2, y: 2, z: 4, core: 2. Of those that a mesh axis runs over, the one named last changes fastest.
Arguments:
- w_query: float32 [16384, 4096], P(('shift', 'shard'), 'width'), parts along dimension 0, may hold values from -0.125 to 0.125
- first_query: float32 [16384, 4096], P(('shift', 'shard'), 'width'), parts along dimension 0, may hold values from -0.09375 to 0.09375
- second_query: float32 [16384, 4096], P(('shift', 'shard'), 'width'), parts along dimension 0, may hold values from -0.09375 to 0.09375
- w_key: float32 [16384, 1024], P(('shift', 'shard'), 'width'), parts along dimension 0, may hold values from -0.125 to 0.125
- first_key: float32 [16384, 1024], P(('shift', 'shard'), 'width'), parts along dimension 0, may hold values from -0.09375 to 0.09375
- second_key: float32 [16384, 1024], P(('shift', 'shard'), 'width'), parts along dimension 0, may hold values from -0.09375 to 0.09375
- w_value: float32 [16384, 1024], P(('shift', 'shard'), 'width'), parts along dimension 0, may hold values from -0.125 to 0.125
- first_value: float32 [16384, 1024], P(('shift', 'shard'), 'width'), parts along dimension 0, may hold values from -0.09375 to 0.09375
- second_value: float32 [16384, 1024], P(('shift', 'shard'), 'width'), parts along dimension 0, may hold values from -0.09375 to 0.09375
- norm_gain: float32 [16384], P(('shift', 'shard')), parts along dimension 0, may hold values from 0.25 to 1.75
Outputs:
- ready_query: bfloat16 [16384, 4096], P('shift', 'width'), parts along dimension 0
- ready_key: bfloat16 [16384, 1024], P('shift', 'width'), parts along dimension 0
- ready_value: bfloat16 [16384, 1024], P('shift', 'width'), parts along dimension 0
- scale_query: float32 [16384], P(('shift', 'width')), parts along dimension 0
- scale_key: float32 [4096], P(('shift', 'width')), parts along dimension 0
- scale_value: float32 [4096], P(('shift', 'width')), parts along dimension 0
There are 4 independent parts, one for each index of `shift`. A program takes and returns all parts, laid end to end along the dimension named above; each array names one. Nothing has to cross between parts.
All inputs are finite; a program needn't handle non-finite values. Where the computation divides by a largest or mean magnitude, that divisor is 1e-20 or more.
Results may differ from a plain program's by a relative error of at most 0.001.
Values may be sent and summed in bfloat16 or wider, within the bound.
A program may use at most 128 MiB of HBM per device.

v0:
```python
import jax
import jax.numpy as jnp
from jax import lax
from jax.sharding import PartitionSpec as P

learn_rate = 0.25
hold_rate = 0.8


def body(
    w_query,
    first_query,
    second_query,
    w_key,
    first_key,
    second_key,
    w_value,
    first_value,
    second_value,
    norm_gain,
):
    hold_query = hold_rate * first_query + second_query
    latest_query = w_query - learn_rate * hold_query
    hold_key = hold_rate * first_key + second_key
    latest_key = w_key - learn_rate * hold_key
    hold_value = hold_rate * first_value + second_value
    latest_value = w_value - learn_rate * hold_value
    latest_gained_query = latest_query * norm_gain[:, None]
    latest_gained_key = latest_key * norm_gain[:, None]
    latest_gained_value = latest_value * norm_gain[:, None]
    scale_query, scale_key, scale_value = lax.pmax(
        (
            jnp.max(jnp.abs(latest_gained_query), axis=0),
            jnp.max(jnp.abs(latest_gained_key), axis=0),
            jnp.max(jnp.abs(latest_gained_value), axis=0),
        ),
        "shard",
    )
    narrow_query, narrow_key, narrow_value = (
        (latest_gained_query / scale_query).astype(jnp.bfloat16),
        (latest_gained_key / scale_key).astype(jnp.bfloat16),
        (latest_gained_value / scale_value).astype(jnp.bfloat16),
    )
    ready_query, ready_key, ready_value = (
        lax.all_gather(narrow_query, "shard", axis=0, tiled=True),
        lax.all_gather(narrow_key, "shard", axis=0, tiled=True),
        lax.all_gather(narrow_value, "shard", axis=0, tiled=True),
    )
    return (ready_query, ready_key, ready_value, scale_query, scale_key, scale_value)


def solution(mesh):
    in_specs = (
        P(("shift", "shard"), "width"),
        P(("shift", "shard"), "width"),
        P(("shift", "shard"), "width"),
        P(("shift", "shard"), "width"),
        P(("shift", "shard"), "width"),
        P(("shift", "shard"), "width"),
        P(("shift", "shard"), "width"),
        P(("shift", "shard"), "width"),
        P(("shift", "shard"), "width"),
        P(("shift", "shard")),
    )
    out_specs = (
        P("shift", "width"),
        P("shift", "width"),
        P("shift", "width"),
        P(("shift", "width")),
        P(("shift", "width")),
        P(("shift", "width")),
    )
    return jax.shard_map(body, mesh=mesh, in_specs=in_specs, out_specs=out_specs, check_vma=False)
```

profile of v0, /device:TPU:3, one launch (start us, length us, event | category | flops | bytes accessed | tf_op | source)
XLA Modules:
  0.0 96.3 jit_solution(6725037320216461155)
XLA Ops:
  7.2 0.0 copy-start.8
  7.2 0.0 all-gather.6.cloned.1.call-start
  7.2 0.0 copy-start.2
  7.2 0.0 copy-start.3
  7.2 0.0 copy-start.4
  7.3 0.0 copy-start.5
  7.3 0.0 copy-start.6
  7.3 0.0 copy-start.7
  7.3 12.8 %abs_reduce_fusion = (f32[1024]{0:T(1024)S(1)}, f32[2048,1024]{1,0:T(8,128)}) fusion(f32[2048]{0:T(1024)} %param.19, f32[2048,1024]{1,0:T(8,128)} %param.10, f32[2048,1024]{1,0:T(8,128)} %param.12, f32[2048,1024]{1,0:T(8,128)} %param.11), kind=kLoop, calls=%fused_computation.1 | loop fusion | flops 14679040 | bytes 33566720 | tf_op jit(solution)/shard_map/reduce_max | solution.py:33
  20.1 0.0 copy-done.8
  20.1 0.0 copy-done.2
  20.1 0.0 copy-done.3
  20.1 0.0 copy-done.4
  20.1 0.4 copy-done.5
  20.6 1.0 %copy-done.6 = f32[2048,256]{1,0:T(8,128)S(1)} copy-done((f32[2048,256]{1,0:T(8,128)S(1)}, f32[2048,256]{1,0:T(8,128)}, u32[]{:S(2)}) %copy-start.6) | copy-done | bytes 2097176
  21.6 0.6 copy-done.7
  22.2 1.8 %abs_reduce_fusion.1 = (f32[256]{0:T(256)S(1)}, f32[2048,256]{1,0:T(8,128)S(1)}, f32[256]{0:T(256)S(1)}, f32[2048,256]{1,0:T(8,128)}) fusion(f32[2048]{0:T(1024)S(1)} %copy-done.8, f32[2048,256]{1,0:T(8,128)S(1)} %copy-done.2, f32[2048,256]{1,0:T(8,128)S(1)} %copy-done.3, f32[2048,256]{1,0:T(8,128)S(1)} %copy-done.4, f32[2048,256]{1,0:T(8,128)S(1)} %copy-done.5, ...), kind=kLoop, calls=%fused_computation.4 | loop fusion | flops 7339520 | bytes 16787456 | tf_op jit(solution)/shard_map/reduce_max | solution.py:35
  24.0 2.8 %all-reduce = (f32[1024]{0:T(1024)S(1)}, f32[256]{0:T(256)S(1)}, f32[256]{0:T(256)S(1)}) all-reduce(f32[1024]{0:T(1024)S(1)} %get-tuple-element.13, f32[256]{0:T(256)S(1)} %get-tuple-element.15, f32[256]{0:T(256)S(1)} %get-tuple-element.9), channel_id=1, replica_groups=mesh['shard'=2,'width'=4,'shift'=4] {'shard'}, use_global_device_ids=true, to_apply=%region_1.0 | all-reduce | flops 1536 | bytes 12288 | tf_op jit(solution)/shard_map/pmax | solution.py:31
  26.8 0.0 copy-start.10
  26.8 0.0 copy-start.11
  26.8 0.0 copy-start.9
  26.8 2.7 %divide_convert_fusion.2 = bf16[2048,256]{1,0:T(8,128)(2,1)} fusion(f32[2048,256]{1,0:T(8,128)} %get-tuple-element.16, f32[256]{0:T(256)S(1)} %get-tuple-element.27), kind=kLoop, calls=%fused_computation.6 | loop fusion | flops 1048576 | bytes 3146752 | tf_op jit(solution)/shard_map/convert_element_type | solution.py:41
  29.5 0.0 all-gather.6.cloned.1.call-update
  29.5 0.0 copy-done.10
  29.5 0.0 all-gather.8.cloned.1.call-start
  29.6 0.0 copy-done.11
  29.6 1.1 %divide_convert_fusion.1 = bf16[2048,256]{1,0:T(8,128)(2,1)} fusion(f32[2048,256]{1,0:T(8,128)S(1)} %get-tuple-element.10, f32[256]{0:T(256)S(1)} %get-tuple-element.28), kind=kLoop, calls=%fused_computation.3 | loop fusion | flops 1048576 | bytes 3146752 | tf_op jit(solution)/shard_map/convert_element_type | solution.py:42
  30.7 0.0 all-gather.8.cloned.1.call-update
  30.8 0.0 all-gather.4.cloned.1.call-start
  30.8 0.0 copy-done.9
  30.8 6.6 %divide_convert_fusion = bf16[2048,1024]{1,0:T(8,128)(2,1)} fusion(f32[2048,1024]{1,0:T(8,128)} %get-tuple-element.14, f32[1024]{0:T(1024)S(1)} %get-tuple-element.26), kind=kLoop, calls=%fused_computation | loop fusion | flops 4194304 | bytes 12587008 | tf_op jit(solution)/shard_map/convert_element_type | solution.py:40
  37.4 0.0 all-gather.4.cloned.1.call-update
  37.5 4.4 %all-gather.6.cloned.1.call-done = bf16[4096,256]{1,0:T(8,128)(2,1)} async-done(((bf16[2048,256]{1,0:T(8,128)(2,1)}), bf16[4096,256]{1,0:T(8,128)(2,1)}) %all-gather.6.cloned.1.call-update) | async-done | bytes 2097168 | tf_op jit(solution)/shard_map/all_gather | solution.py:46
  41.9 0.0 copy-start
  41.9 13.9 %all-gather.8.cloned.1.call-done = bf16[4096,256]{1,0:T(8,128)(2,1)} async-done(((bf16[2048,256]{1,0:T(8,128)(2,1)}), bf16[4096,256]{1,0:T(8,128)(2,1)}) %all-gather.8.cloned.1.call-update) | async-done | bytes 2097168 | tf_op jit(solution)/shard_map/all_gather | solution.py:47
  55.8 22.6 %all-gather.4.cloned.1.call-done = bf16[4096,1024]{1,0:T(8,128)(2,1)} async-done(((bf16[2048,1024]{1,0:T(8,128)(2,1)}), bf16[4096,1024]{1,0:T(8,128)(2,1)}) %all-gather.4.cloned.1.call-update) | async-done | bytes 8388624 | tf_op jit(solution)/shard_map/all_gather | solution.py:45
  78.4 7.8 %copy.19 = bf16[4096,1024]{1,0:T(8,128)(2,1)} copy(bf16[4096,1024]{1,0:T(8,128)(2,1)} %all-gather.4.cloned.1.call-done) | data formatting | bytes 16777216
  86.1 0.0 copy-done
  86.1 0.0 copy-start.1
  86.1 1.3 %copy.20 = bf16[4096,256]{1,0:T(8,128)(2,1)} copy(bf16[4096,256]{1,0:T(8,128)(2,1)S(1)} %copy-done) | data formatting | bytes 4194304
  87.5 1.0 %copy-done.1 = bf16[4096,256]{1,0:T(8,128)(2,1)S(1)} copy-done((bf16[4096,256]{1,0:T(8,128)(2,1)S(1)}, bf16[4096,256]{1,0:T(8,128)(2,1)}, u32[]{:S(2)}) %copy-start.1) | copy-done | bytes 2097176
  88.5 1.3 %copy.21 = bf16[4096,256]{1,0:T(8,128)(2,1)} copy(bf16[4096,256]{1,0:T(8,128)(2,1)S(1)} %copy-done.1) | data formatting | bytes 4194304
Async XLA Ops:
  7.2 13.0 %copy-start.8 = (f32[2048]{0:T(1024)S(1)}, f32[2048]{0:T(1024)}, u32[]{:S(2)}) copy-start(f32[2048]{0:T(1024)} %param.19) | copy-start | bytes 24580
  7.2 34.7 %all-gather.6.cloned.1.call-start = ((), (), s32[]{:S(2)}) async-start(), calls=%async_computation.1 | async-start | bytes 3145728 | tf_op jit(solution)/shard_map/all_gather | solution.py:46
  7.2 12.9 %copy-start.2 = (f32[2048,256]{1,0:T(8,128)S(1)}, f32[2048,256]{1,0:T(8,128)}, u32[]{:S(2)}) copy-start(f32[2048,256]{1,0:T(8,128)} %param.16) | copy-start | bytes 6291460
  7.2 12.9 %copy-start.3 = (f32[2048,256]{1,0:T(8,128)S(1)}, f32[2048,256]{1,0:T(8,128)}, u32[]{:S(2)}) copy-start(f32[2048,256]{1,0:T(8,128)} %param.18) | copy-start | bytes 6291460
  7.2 12.9 %copy-start.4 = (f32[2048,256]{1,0:T(8,128)S(1)}, f32[2048,256]{1,0:T(8,128)}, u32[]{:S(2)}) copy-start(f32[2048,256]{1,0:T(8,128)} %param.17) | copy-start | bytes 6291460
  7.3 13.3 %copy-start.5 = (f32[2048,256]{1,0:T(8,128)S(1)}, f32[2048,256]{1,0:T(8,128)}, u32[]{:S(2)}) copy-start(f32[2048,256]{1,0:T(8,128)} %param.13) | copy-start | bytes 6291460
  7.3 14.3 %copy-start.6 = (f32[2048,256]{1,0:T(8,128)S(1)}, f32[2048,256]{1,0:T(8,128)}, u32[]{:S(2)}) copy-start(f32[2048,256]{1,0:T(8,128)} %param.15) | copy-start | bytes 6291460
  7.3 14.9 %copy-start.7 = (f32[2048,256]{1,0:T(8,128)S(1)}, f32[2048,256]{1,0:T(8,128)}, u32[]{:S(2)}) copy-start(f32[2048,256]{1,0:T(8,128)} %param.14) | copy-start | bytes 6291460
  26.8 2.8 %copy-start.10 = (f32[256]{0:T(256)}, f32[256]{0:T(256)S(1)}, u32[]{:S(2)}) copy-start(f32[256]{0:T(256)S(1)} %get-tuple-element.27) | copy-start | bytes 3076
  26.8 2.8 %copy-start.11 = (f32[256]{0:T(256)}, f32[256]{0:T(256)S(1)}, u32[]{:S(2)}) copy-start(f32[256]{0:T(256)S(1)} %get-tuple-element.28) | copy-start | bytes 3076
  26.8 4.0 %copy-start.9 = (f32[1024]{0:T(1024)}, f32[1024]{0:T(1024)S(1)}, u32[]{:S(2)}) copy-start(f32[1024]{0:T(1024)S(1)} %get-tuple-element.26) | copy-start | bytes 12292
  29.5 26.2 %all-gather.8.cloned.1.call-start = ((), (), s32[]{:S(2)}) async-start(), calls=%async_computation.2 | async-start | bytes 3145728 | tf_op jit(solution)/shard_map/all_gather | solution.py:47
  30.8 47.6 %all-gather.4.cloned.1.call-start = ((), (), s32[]{:S(2)}) async-start(), calls=%async_computation | async-start | bytes 12582912 | tf_op jit(solution)/shard_map/all_gather | solution.py:45
  41.9 44.3 %copy-start = (bf16[4096,256]{1,0:T(8,128)(2,1)S(1)}, bf16[4096,256]{1,0:T(8,128)(2,1)}, u32[]{:S(2)}) copy-start(bf16[4096,256]{1,0:T(8,128)(2,1)} %all-gather.6.cloned.1.call-done) | copy-start | bytes 6291460
  86.1 2.3 %copy-start.1 = (bf16[4096,256]{1,0:T(8,128)(2,1)S(1)}, bf16[4096,256]{1,0:T(8,128)(2,1)}, u32[]{:S(2)}) copy-start(bf16[4096,256]{1,0:T(8,128)(2,1)} %all-gather.8.cloned.1.call-done) | copy-start | bytes 6291460
Sparse Core Ops, SparseCore 0:
  29.6 12.1 all-gather.5
  44.0 11.7 all-gather.7
  57.3 21.0 all-gather.3
where the time goes:
time: 97.4 us; the launch traced here: 96.3 us
  waiting for transfers between devices  41 us (42%)
  other arithmetic  25.1 us (26%)
  between operations  13.9 us (14%)
  local copies, waits for them, and re-layouts  13.5 us (14%)
  blocking collectives  2.79 us (3%)
    all_gather x1, waiting for transfers between devices, body(): lax.all_gather(narrow_query, 'shard', axis=0, tiled=True)  22.6 us
    all_gather x1, waiting for transfers between devices, body(): lax.all_gather(narrow_value, 'shard', axis=0, tiled=True)  13.9 us
    unnamed x27, local copies, waits for them, and re-layouts  13.5 us
    reduce_max x1, other arithmetic, body(): jnp.max(jnp.abs(latest_gained_query), axis=0)  12.8 us
    convert_element_type x1, other arithmetic, body(): (latest_gained_query / scale_query).astype(jnp.bfloat16)  6.62 us
    all_gather x1, waiting for transfers between devices, body(): lax.all_gather(narrow_key, 'shard', axis=0, tiled=True)  4.42 us
    pmax x1, blocking collectives, body(): lax.pmax((jnp.max(jnp.abs(latest_gained_query), axis=0), jnp.max(jnp.abs(...  2.79 us
    convert_element_type x1, other arithmetic, body(): (latest_gained_key / scale_key).astype(jnp.bfloat16)  2.73 us
  transfers between devices with their start and end apart: 3, of which 3 were waited for; matrix products, arithmetic and copies ran while one was open for 8% of the time, Pallas kernels for 0%

commit v1 on v0

v1 whole, which is shorter than its diff:
```python
import functools

import jax
import jax.numpy as jnp
from jax import lax
from jax.experimental import pallas as pl
from jax.experimental.pallas import tpu as pltpu
from jax.sharding import PartitionSpec as P

learn_rate = 0.25
hold_rate = 0.8

LANES = 128
SUBLANES = 8
STEP_ROWS = 128
AHEAD = 6
MESH = pl.DeviceIdType.MESH


def exchange_kernel(peers, chunks, *refs):
    gain_ref, sources, readies, scales = refs[0], refs[1:10], refs[10:13], refs[13:16]
    held, gains, peaks, arrived, in_sem, peak_send, peak_recv, out_send, out_recv = refs[16:]
    rows = gains.shape[0]
    me = lax.axis_index("shard")
    others = [lax.rem(me + k, peers) for k in range(1, peers)]
    my_rows = pl.ds(pl.multiple_of(me * rows, rows), rows)

    def reads(c):
        which, col = chunks[c]
        return [
            pltpu.make_async_copy(
                sources[3 * which + i].at[:, pl.ds(col * LANES, LANES)],
                held.at[i, c],
                in_sem.at[i, c],
            )
            for i in range(3)
        ]

    for c in range(min(AHEAD, len(chunks))):
        for read in reads(c):
            read.start()

    barrier = pltpu.get_barrier_semaphore()
    for other in others:
        pl.semaphore_signal(barrier, inc=1, device_id={"shard": other}, device_id_type=MESH)

    for j in range(rows // LANES):
        spread = jnp.broadcast_to(gain_ref[pl.ds(j, 1), :], (LANES, LANES))
        gains[pl.ds(j * LANES, LANES), :] = spread.T

    pl.semaphore_wait(barrier, peers - 1)

    def update(c):
        def step(r, peak):
            here = pl.ds(pl.multiple_of(r * STEP_ROWS, STEP_ROWS), STEP_ROWS)
            hold = hold_rate * held[1, c, here, :] + held[2, c, here, :]
            gained = (held[0, c, here, :] - learn_rate * hold) * gains[here, :]
            held[0, c, here, :] = gained
            tiles = jnp.abs(gained).reshape(STEP_ROWS // SUBLANES, SUBLANES, LANES)
            return jnp.maximum(peak, jnp.max(tiles, axis=0))

        peaks[c] = lax.fori_loop(
            0, rows // STEP_ROWS, step, jnp.zeros((SUBLANES, LANES), jnp.float32)
        )

    def peak_copy(c, k):
        return pltpu.make_async_remote_copy(
            src_ref=peaks.at[c],
            dst_ref=arrived.at[k, c],
            send_sem=peak_send.at[k, c],
            recv_sem=peak_recv.at[k, c],
            device_id={"shard": others[k]},
            device_id_type=MESH,
        )

    def scale_and_round(c):
        which, col = chunks[c]
        peak = peaks[c]
        for k in range(peers - 1):
            peak_copy(c, k).wait_recv()
            peak = jnp.maximum(peak, arrived[k, c])
        scale = jnp.max(peak, axis=0, keepdims=True)
        scales[which][pl.ds(col, 1), :] = scale
        inverse = jnp.broadcast_to(1.0 / scale, (STEP_ROWS, LANES))
        columns = pl.ds(col * LANES, LANES)

        def step(r, _):
            here = pl.ds(pl.multiple_of(r * STEP_ROWS, STEP_ROWS), STEP_ROWS)
            there = pl.ds(pl.multiple_of(me * rows + r * STEP_ROWS, STEP_ROWS), STEP_ROWS)
            readies[which][there, columns] = (held[0, c, here, :] * inverse).astype(jnp.bfloat16)
            return 0

        lax.fori_loop(0, rows // STEP_ROWS, step, 0)

    def out_copy(c, k):
        which, col = chunks[c]
        block = readies[which].at[my_rows, pl.ds(col * LANES, LANES)]
        return pltpu.make_async_remote_copy(
            src_ref=block,
            dst_ref=block,
            send_sem=out_send.at[k, c],
            recv_sem=out_recv.at[k, c],
            device_id={"shard": others[k]},
            device_id_type=MESH,
        )

    for c in range(len(chunks) + 1):
        if c < len(chunks):
            for read in reads(c):
                read.wait()
            if c + AHEAD < len(chunks):
                for read in reads(c + AHEAD):
                    read.start()
            update(c)
            for k in range(peers - 1):
                peak_copy(c, k).start()
        if c >= 1:
            scale_and_round(c - 1)
            for k in range(peers - 1):
                out_copy(c - 1, k).start()

    for c in range(len(chunks)):
        for k in range(peers - 1):
            peak_copy(c, k).wait_send()
            out_copy(c, k).wait_send()
            out_copy(c, k).wait_recv()


def store_kernel(pieces, *refs):
    half = len(refs) // 2
    sources, targets, sem = refs[:half], refs[half : 2 * half], refs[-1]
    copies = []
    for source, target in zip(sources, targets):
        parts = pieces if source.shape[0] % (pieces * LANES) == 0 else 1
        size = source.shape[0] // parts
        for p in range(parts):
            where = pl.ds(p * size, size)
            copies.append(
                pltpu.make_async_copy(source.at[where], target.at[where], sem.at[len(copies)])
            )
    for copy in copies:
        copy.start()
    for copy in copies:
        copy.wait()


def body(*arrays):
    *weights, norm_gain = arrays
    peers = lax.axis_size("shard")
    rows = norm_gain.shape[0]
    widths = [weights[3 * which].shape[1] for which in range(3)]
    chunks = [(which, col) for which in range(3) for col in range(widths[which] // LANES)]
    count = len(chunks)
    any_spec = pl.BlockSpec(memory_space=pltpu.HBM)
    vmem_spec = pl.BlockSpec(memory_space=pltpu.VMEM)
    ready_shapes = [((peers * rows, width), jnp.bfloat16) for width in widths]
    scale_shapes = [((width // LANES, LANES), jnp.float32) for width in widths]
    made = pl.pallas_call(
        functools.partial(exchange_kernel, peers, chunks),
        out_shape=[pltpu.VMEM(*s) for s in ready_shapes + scale_shapes],
        in_specs=[vmem_spec] + [any_spec] * 9,
        out_specs=[vmem_spec] * 6,
        scratch_shapes=[
            pltpu.VMEM((3, count, rows, LANES), jnp.float32),
            pltpu.VMEM((rows, LANES), jnp.float32),
            pltpu.VMEM((count, SUBLANES, LANES), jnp.float32),
            pltpu.VMEM((peers - 1, count, SUBLANES, LANES), jnp.float32),
            pltpu.SemaphoreType.DMA((3, count)),
            pltpu.SemaphoreType.DMA((peers - 1, count)),
            pltpu.SemaphoreType.DMA((peers - 1, count)),
            pltpu.SemaphoreType.DMA((peers - 1, count)),
            pltpu.SemaphoreType.DMA((peers - 1, count)),
        ],
        compiler_params=pltpu.CompilerParams(
            collective_id=0, has_side_effects=True, vmem_limit_bytes=44 * 1024 * 1024
        ),
        name="exchange",
    )(norm_gain.reshape(rows // LANES, LANES), *weights)
    pieces = 4
    stored = pl.pallas_call(
        functools.partial(store_kernel, pieces),
        out_shape=[jax.ShapeDtypeStruct(*s) for s in ready_shapes + scale_shapes],
        in_specs=[vmem_spec] * 6,
        out_specs=[any_spec] * 6,
        scratch_shapes=[pltpu.SemaphoreType.DMA((6 * pieces,))],
        compiler_params=pltpu.CompilerParams(vmem_limit_bytes=2 * 1024 * 1024),
        name="store",
    )(*made)
    return (*stored[:3], *(s.reshape(-1) for s in stored[3:]))


def solution(mesh):
    split = P(("shift", "shard"), "width")
    in_specs = (split,) * 9 + (P(("shift", "shard")),)
    out_specs = (P("shift", "width"),) * 3 + (P(("shift", "width")),) * 3
    return jax.shard_map(body, mesh=mesh, in_specs=in_specs, out_specs=out_specs, check_vma=False)
```

time: 97.4 us -> 23 us (0.24)
  waiting for transfers between devices: 41 us -> 0 us
  other arithmetic: 25.1 us -> 0 us
  Pallas kernels: 0 us -> 22.1 us
  local copies, waits for them, and re-layouts: 13.5 us -> 0 us
  between operations: 13.9 us -> 0.64 us
  blocking collectives: 2.79 us -> 0 us
    all_gather x3 -> x0, waiting for transfers between devices: 40.9 us -> none  [the longest x1 22.6 us: body(): lax.all_gather(narrow_query, 'shard', axis=0, tiled=True)]
    pallas_call x0 -> x2, Pallas kernels: none -> 22.1 us  [the longest x1 17.4 us: body(): pl.pallas_call(functools.partial(exchange_kernel, peers, chunks), out_sha...]
    reduce_max x2 -> x0, other arithmetic: 14.6 us -> none  [the longest x1 12.8 us: body(): jnp.max(jnp.abs(latest_gained_query), axis=0)]
    unnamed x27 -> x0, local copies, waits for them, and re-layouts: 13.5 us -> none
    convert_element_type x3 -> x0, other arithmetic: 10.5 us -> none  [the longest x1 6.62 us: body(): (latest_gained_query / scale_query).astype(jnp.bfloat16)]
    pmax x1 -> x0, blocking collectives: 2.79 us -> none  [body(): lax.pmax((jnp.max(jnp.abs(latest_gained_query), axis=0), jnp.max(jnp.abs(...]
  transfers between devices with their start and end apart: 3 -> 0, of which waited for: 3 -> 0; matrix products, arithmetic and copies ran while one was open for 8% -> 0% of each run, Pallas kernels for 0% -> 0%
where the time goes in v1:
time: 23 us; the launch traced here: 22.8 us
  Pallas kernels  22.1 us (96%)
  between operations  0.64 us (3%)
    pallas_call x1, Pallas kernels, body(): pl.pallas_call(functools.partial(exchange_kernel, peers, chunks), out_sha...  17.4 us
    pallas_call x1, Pallas kernels, body(): pl.pallas_call(functools.partial(store_kernel, pieces), out_shape=[jax.Sh...  4.76 us

profile of v1, /device:TPU:3, one launch (start us, length us, event | category | flops | bytes accessed | tf_op | source)
XLA Modules:
  0.0 22.8 jit_solution(12293555880581984486)
XLA Ops:
  0.6 17.4 %exchange.1 = (bf16[4096,1024]{1,0:T(8,128)(2,1)S(1)}, bf16[4096,256]{1,0:T(8,128)(2,1)S(1)}, bf16[4096,256]{1,0:T(8,128)(2,1)S(1)}, f32[8,128]{1,0:T(8,128)S(1)...) custom-call(f32[16,128]{1,0:T(8,128)} %bitcast.4, f32[2048,1024]{1,0:T(8,128)} %refs_1_.1, f32[2048,1024]{1,0:T(8,128)} %refs_2_.1, ...), custom_call_target="tpu_custom_call" | custom-call | tf_op jit(solution)/shard_map/exchange/pallas_call | solution.py:158
  18.0 4.8 %store.1 = (bf16[4096,1024]{1,0:T(8,128)(2,1)}, bf16[4096,256]{1,0:T(8,128)(2,1)}, bf16[4096,256]{1,0:T(8,128)(2,1)}, f32[8,128]{1,0:T(8,128)}, f32[2,128]{1,0:T(2,128)}, /*index=5*/f32[2,128]{1,0:T(2,128)}) custom-call(bf16[4096,1024]{1,0:T(8,128)(2,1)S(1)} %get-tuple-element.18.refs_0_, bf16[4096,256]{1,0:T(8,128)(2,1)S(1)} %get-tuple-element.19.refs_1_, ...), custom_call_target="tpu_custom_call" | custom-call | tf_op jit(solution)/shard_map/store/pallas_call | solution.py:180

commit v2 on v1

--- a/solution.py
+++ b/solution.py
@@ -12,45 +12,60 @@
 
 LANES = 128
 SUBLANES = 8
-STEP_ROWS = 128
-AHEAD = 6
+STEP_ROWS = 64
+AHEAD = 12
+PIECES = 4
 MESH = pl.DeviceIdType.MESH
 
 
 def exchange_kernel(peers, chunks, *refs):
     gain_ref, sources, readies, scales = refs[0], refs[1:10], refs[10:13], refs[13:16]
-    held, gains, peaks, arrived, in_sem, peak_send, peak_recv, out_send, out_recv = refs[16:]
+    gain_held, held, gains, peaks, arrived, gain_sem, in_sem, peak_send, peak_recv, out_send, out_recv = refs[16:]
     rows = gains.shape[0]
     me = lax.axis_index("shard")
     others = [lax.rem(me + k, peers) for k in range(1, peers)]
     my_rows = pl.ds(pl.multiple_of(me * rows, rows), rows)
 
-    def reads(c):
+    last = len(chunks) - 1
+    piece_rows = rows // PIECES
+
+    def reads(c, piece=None):
         which, col = chunks[c]
+        some = pl.ds(0, rows) if piece is None else pl.ds(piece * piece_rows, piece_rows)
         return [
             pltpu.make_async_copy(
-                sources[3 * which + i].at[:, pl.ds(col * LANES, LANES)],
-                held.at[i, c],
-                in_sem.at[i, c],
+                sources[3 * which + i].at[some, pl.ds(col * LANES, LANES)],
+                held.at[i, c, some],
+                in_sem.at[i, c + (piece or 0)],
             )
             for i in range(3)
         ]
 
-    for c in range(min(AHEAD, len(chunks))):
-        for read in reads(c):
-            read.start()
+    def start_reads(c):
+        for piece in range(PIECES) if c == last else (None,):
+            for read in reads(c, piece):
+                read.start()
+
+    gain_read = pltpu.make_async_copy(gain_ref, gain_held, gain_sem)
+    gain_read.start()
+
+    for c in range(min(1, len(chunks))):
+        start_reads(c)
 
     barrier = pltpu.get_barrier_semaphore()
     for other in others:
         pl.semaphore_signal(barrier, inc=1, device_id={"shard": other}, device_id_type=MESH)
 
+    gain_read.wait()
+    for c in range(min(1, len(chunks)), min(AHEAD, len(chunks))):
+        start_reads(c)
     for j in range(rows // LANES):
-        spread = jnp.broadcast_to(gain_ref[pl.ds(j, 1), :], (LANES, LANES))
+        spread = jnp.broadcast_to(gain_held[pl.ds(j, 1), :], (LANES, LANES))
         gains[pl.ds(j * LANES, LANES), :] = spread.T
 
     pl.semaphore_wait(barrier, peers - 1)
 
-    def update(c):
+    def update(c, first, count, peak):
         def step(r, peak):
             here = pl.ds(pl.multiple_of(r * STEP_ROWS, STEP_ROWS), STEP_ROWS)
             hold = hold_rate * held[1, c, here, :] + held[2, c, here, :]
@@ -59,9 +74,7 @@
             tiles = jnp.abs(gained).reshape(STEP_ROWS // SUBLANES, SUBLANES, LANES)
             return jnp.maximum(peak, jnp.max(tiles, axis=0))
 
-        peaks[c] = lax.fori_loop(
-            0, rows // STEP_ROWS, step, jnp.zeros((SUBLANES, LANES), jnp.float32)
-        )
+        return lax.fori_loop(first // STEP_ROWS, (first + count) // STEP_ROWS, step, peak)
 
     def peak_copy(c, k):
         return pltpu.make_async_remote_copy(
@@ -90,11 +103,18 @@
             readies[which][there, columns] = (held[0, c, here, :] * inverse).astype(jnp.bfloat16)
             return 0
 
-        lax.fori_loop(0, rows // STEP_ROWS, step, 0)
-
-    def out_copy(c, k):
+        for piece in range(PIECES):
+            first = piece * piece_rows
+            lax.fori_loop(first // STEP_ROWS, (first + piece_rows) // STEP_ROWS, step, 0)
+            for k in range(peers - 1):
+                out_copy(c, k, piece).start()
+
+    def out_copy(c, k, piece=None):
         which, col = chunks[c]
-        block = readies[which].at[my_rows, pl.ds(col * LANES, LANES)]
+        some = my_rows
+        if piece is not None:
+            some = pl.ds(pl.multiple_of(me * rows + piece * piece_rows, piece_rows), piece_rows)
+        block = readies[which].at[some, pl.ds(col * LANES, LANES)]
         return pltpu.make_async_remote_copy(
             src_ref=block,
             dst_ref=block,
@@ -106,18 +126,23 @@
 
     for c in range(len(chunks) + 1):
         if c < len(chunks):
-            for read in reads(c):
-                read.wait()
-            if c + AHEAD < len(chunks):
-                for read in reads(c + AHEAD):
-                    read.start()
-            update(c)
+            peak = jnp.zeros((SUBLANES, LANES), jnp.float32)
+            if c == last:
+                for piece in range(PIECES):
+                    for read in reads(c, piece):
+                        read.wait()
+                    peak = update(c, piece * piece_rows, piece_rows, peak)
+            else:
+                for read in reads(c):
+                    read.wait()
+                if c + AHEAD <= last:
+                    start_reads(c + AHEAD)
+                peak = update(c, 0, rows, peak)
+            peaks[c] = peak
             for k in range(peers - 1):
                 peak_copy(c, k).start()
         if c >= 1:
             scale_and_round(c - 1)
-            for k in range(peers - 1):
-                out_copy(c - 1, k).start()
 
     for c in range(len(chunks)):
         for k in range(peers - 1):
@@ -158,14 +183,16 @@
     made = pl.pallas_call(
         functools.partial(exchange_kernel, peers, chunks),
         out_shape=[pltpu.VMEM(*s) for s in ready_shapes + scale_shapes],
-        in_specs=[vmem_spec] + [any_spec] * 9,
+        in_specs=[any_spec] * 10,
         out_specs=[vmem_spec] * 6,
         scratch_shapes=[
+            pltpu.VMEM((rows // LANES, LANES), jnp.float32),
             pltpu.VMEM((3, count, rows, LANES), jnp.float32),
             pltpu.VMEM((rows, LANES), jnp.float32),
             pltpu.VMEM((count, SUBLANES, LANES), jnp.float32),
             pltpu.VMEM((peers - 1, count, SUBLANES, LANES), jnp.float32),
-            pltpu.SemaphoreType.DMA((3, count)),
+            pltpu.SemaphoreType.DMA,
+            pltpu.SemaphoreType.DMA((3, count + PIECES - 1)),
             pltpu.SemaphoreType.DMA((peers - 1, count)),
             pltpu.SemaphoreType.DMA((peers - 1, count)),
             pltpu.SemaphoreType.DMA((peers - 1, count)),
@@ -176,7 +203,7 @@
         ),
         name="exchange",
     )(norm_gain.reshape(rows // LANES, LANES), *weights)
-    pieces = 4
+    pieces = 2
     stored = pl.pallas_call(
         functools.partial(store_kernel, pieces),
         out_shape=[jax.ShapeDtypeStruct(*s) for s in ready_shapes + scale_shapes],

time: 23 us -> 22.5 us (0.978)
  Pallas kernels: 22.1 us -> 21.7 us
    pallas_call x1, Pallas kernels: 17.4 us -> 17 us  [body(): pl.pallas_call(functools.partial(exchange_kernel, peers, chunks), out_sha...]
where the time goes in v2:
time: 22.5 us; the launch traced here: 22.3 us
  Pallas kernels  21.7 us (96%)
  between operations  0.64 us (3%)
    pallas_call x1, Pallas kernels, body(): pl.pallas_call(functools.partial(exchange_kernel, peers, chunks), out_sha...  17 us
    pallas_call x1, Pallas kernels, body(): pl.pallas_call(functools.partial(store_kernel, pieces), out_shape=[jax.Sh...  4.67 us

profile of v2, /device:TPU:3, one launch (start us, length us, event | category | flops | bytes accessed | tf_op | source)
XLA Modules:
  0.0 22.3 jit_solution(4914658489846797491)
XLA Ops:
  0.6 17.0 %exchange.1 = (bf16[4096,1024]{1,0:T(8,128)(2,1)S(1)}, bf16[4096,256]{1,0:T(8,128)(2,1)S(1)}, bf16[4096,256]{1,0:T(8,128)(2,1)S(1)}, f32[8,128]{1,0:T(8,128)S(1)...) custom-call(f32[16,128]{1,0:T(8,128)} %bitcast.4, f32[2048,1024]{1,0:T(8,128)} %refs_1_.1, f32[2048,1024]{1,0:T(8,128)} %refs_2_.1, ...), custom_call_target="tpu_custom_call" | custom-call | tf_op jit(solution)/shard_map/exchange/pallas_call | solution.py:183
  17.6 4.7 %store.1 = (bf16[4096,1024]{1,0:T(8,128)(2,1)}, bf16[4096,256]{1,0:T(8,128)(2,1)}, bf16[4096,256]{1,0:T(8,128)(2,1)}, f32[8,128]{1,0:T(8,128)}, f32[2,128]{1,0:T(2,128)}, /*index=5*/f32[2,128]{1,0:T(2,128)}) custom-call(bf16[4096,1024]{1,0:T(8,128)(2,1)S(1)} %get-tuple-element.18.refs_0_, bf16[4096,256]{1,0:T(8,128)(2,1)S(1)} %get-tuple-element.19.refs_1_, ...), custom_call_target="tpu_custom_call" | custom-call | tf_op jit(solution)/shard_map/store/pallas_call | solution.py:207

commit v3 on v2

--- a/solution.py
+++ b/solution.py
@@ -12,7 +12,7 @@
 
 LANES = 128
 SUBLANES = 8
-STEP_ROWS = 64
+STEP_ROWS = 128
 AHEAD = 12
 PIECES = 4
 MESH = pl.DeviceIdType.MESH
@@ -28,6 +28,7 @@
 
     last = len(chunks) - 1
     piece_rows = rows // PIECES
+    step_rows = min(STEP_ROWS, piece_rows)
 
     def reads(c, piece=None):
         which, col = chunks[c]
@@ -49,32 +50,30 @@
     gain_read = pltpu.make_async_copy(gain_ref, gain_held, gain_sem)
     gain_read.start()
 
-    for c in range(min(1, len(chunks))):
-        start_reads(c)
-
     barrier = pltpu.get_barrier_semaphore()
     for other in others:
         pl.semaphore_signal(barrier, inc=1, device_id={"shard": other}, device_id_type=MESH)
 
+    pl.semaphore_wait(barrier, peers - 1)
+    for c in range(min(AHEAD, len(chunks))):
+        start_reads(c)
+
     gain_read.wait()
-    for c in range(min(1, len(chunks)), min(AHEAD, len(chunks))):
-        start_reads(c)
     for j in range(rows // LANES):
         spread = jnp.broadcast_to(gain_held[pl.ds(j, 1), :], (LANES, LANES))
         gains[pl.ds(j * LANES, LANES), :] = spread.T
 
-    pl.semaphore_wait(barrier, peers - 1)
 
     def update(c, first, count, peak):
         def step(r, peak):
-            here = pl.ds(pl.multiple_of(r * STEP_ROWS, STEP_ROWS), STEP_ROWS)
+            here = pl.ds(pl.multiple_of(r * step_rows, step_rows), step_rows)
             hold = hold_rate * held[1, c, here, :] + held[2, c, here, :]
             gained = (held[0, c, here, :] - learn_rate * hold) * gains[here, :]
             held[0, c, here, :] = gained
-            tiles = jnp.abs(gained).reshape(STEP_ROWS // SUBLANES, SUBLANES, LANES)
+            tiles = jnp.abs(gained).reshape(step_rows // SUBLANES, SUBLANES, LANES)
             return jnp.maximum(peak, jnp.max(tiles, axis=0))
 
-        return lax.fori_loop(first // STEP_ROWS, (first + count) // STEP_ROWS, step, peak)
+        return lax.fori_loop(first // step_rows, (first + count) // step_rows, step, peak)
 
     def peak_copy(c, k):
         return pltpu.make_async_remote_copy(
@@ -94,18 +93,18 @@
             peak = jnp.maximum(peak, arrived[k, c])
         scale = jnp.max(peak, axis=0, keepdims=True)
         scales[which][pl.ds(col, 1), :] = scale
-        inverse = jnp.broadcast_to(1.0 / scale, (STEP_ROWS, LANES))
+        inverse = jnp.broadcast_to(1.0 / scale, (step_rows, LANES))
         columns = pl.ds(col * LANES, LANES)
 
         def step(r, _):
-            here = pl.ds(pl.multiple_of(r * STEP_ROWS, STEP_ROWS), STEP_ROWS)
-            there = pl.ds(pl.multiple_of(me * rows + r * STEP_ROWS, STEP_ROWS), STEP_ROWS)
+            here = pl.ds(pl.multiple_of(r * step_rows, step_rows), step_rows)
+            there = pl.ds(pl.multiple_of(me * rows + r * step_rows, step_rows), step_rows)
             readies[which][there, columns] = (held[0, c, here, :] * inverse).astype(jnp.bfloat16)
             return 0
 
         for piece in range(PIECES):
             first = piece * piece_rows
-            lax.fori_loop(first // STEP_ROWS, (first + piece_rows) // STEP_ROWS, step, 0)
+            lax.fori_loop(first // step_rows, (first + piece_rows) // step_rows, step, 0)
             for k in range(peers - 1):
                 out_copy(c, k, piece).start()
 

time: 22.5 us -> 22.1 us (0.982)
  Pallas kernels: 21.7 us -> 21.2 us
    pallas_call x1, Pallas kernels: 17 us -> 16.5 us  [body(): pl.pallas_call(functools.partial(exchange_kernel, peers, chunks), out_sha...]
where the time goes in v3:
time: 22.1 us; the launch traced here: 21.9 us
  Pallas kernels  21.2 us (96%)
  between operations  0.64 us (3%)
    pallas_call x1, Pallas kernels, body(): pl.pallas_call(functools.partial(exchange_kernel, peers, chunks), out_sha...  16.5 us
    pallas_call x1, Pallas kernels, body(): pl.pallas_call(functools.partial(store_kernel, pieces), out_shape=[jax.Sh...  4.67 us

profile of v3, /device:TPU:3, one launch (start us, length us, event | category | flops | bytes accessed | tf_op | source)
XLA Modules:
  0.0 21.9 jit_solution(10660201248049301381)
XLA Ops:
  0.6 16.5 %exchange.1 = (bf16[4096,1024]{1,0:T(8,128)(2,1)S(1)}, bf16[4096,256]{1,0:T(8,128)(2,1)S(1)}, bf16[4096,256]{1,0:T(8,128)(2,1)S(1)}, f32[8,128]{1,0:T(8,128)S(1)...) custom-call(f32[16,128]{1,0:T(8,128)} %bitcast.4, f32[2048,1024]{1,0:T(8,128)} %refs_1_.1, f32[2048,1024]{1,0:T(8,128)} %refs_2_.1, ...), custom_call_target="tpu_custom_call" | custom-call | tf_op jit(solution)/shard_map/exchange/pallas_call | solution.py:182
  17.2 4.7 %store.1 = (bf16[4096,1024]{1,0:T(8,128)(2,1)}, bf16[4096,256]{1,0:T(8,128)(2,1)}, bf16[4096,256]{1,0:T(8,128)(2,1)}, f32[8,128]{1,0:T(8,128)}, f32[2,128]{1,0:T(2,128)}, /*index=5*/f32[2,128]{1,0:T(2,128)}) custom-call(bf16[4096,1024]{1,0:T(8,128)(2,1)S(1)} %get-tuple-element.18.refs_0_, bf16[4096,256]{1,0:T(8,128)(2,1)S(1)} %get-tuple-element.19.refs_1_, ...), custom_call_target="tpu_custom_call" | custom-call | tf_op jit(solution)/shard_map/store/pallas_call | solution.py:206
